TPU v7x, 512 devices: a whole 4x8x8 slice. The times are simulated.
512 devices in a mesh: grid: 32 (over y, x), band: 16 (over z, core).
Axes of the slice: x: 4, y: 8, z: 8, core: 2. Of those that a mesh axis runs over, the one named last changes fastest.
Arguments:
- start: float32 [1, 4, 1, 64, 32768], P(None, None, None, 'band', 'grid'), may hold values from -6 to 6
- energies: float32 [4, 64, 32768], P(None, 'band', 'grid'), may hold values from -4 to 4
- sites: int32 [3, 1], replicated, may hold values from 0 to 31
- potential: float32 [32, 32, 32], replicated, may hold values from -4 to 400
Outputs:
- alphas: float32 [1, 1, 4], replicated
- betas: float32 [1, 1, 4], replicated
- lanczos: float32 [1, 4, 1, 64, 32768], P(None, None, None, 'band', 'grid')
All inputs are finite; a program needn't handle non-finite values.
Results may differ from a plain program's by a relative error of at most 0.0003.
Values sent between devices are 32-bit elements; how exact they have to be, the bound alone decides.
A program may use at most 64 MiB of HBM per device.

v0:
```python
import functools
import math

import jax
import jax.numpy as jnp
from jax import lax
from jax.sharding import Mesh
from jax.sharding import PartitionSpec as P

ITERS = 4
GRID = ("grid_0", "grid_1")
BAND = ("band_0", "band_1")
GRID_BAND = ("grid_0", "grid_1", "band_0", "band_1")


precise_mode = lax.Precision.HIGHEST


def one_axis_at_a_time(x, axes):
    return functools.reduce(lax.psum, axes, x)


def cas_table(grid_size):
    cells = jnp.arange(grid_size, dtype=jnp.int32)
    phase = cells[:, None] * cells[None, :] % grid_size
    angle = phase.astype(jnp.float32) * (2.0 * math.pi / grid_size)
    return jnp.cos(angle) + jnp.sin(angle)


def shift_axis(field_part, offset, axis_number):
    length = field_part.shape[axis_number]
    doubled = jnp.concatenate([field_part, field_part], axis=axis_number)
    first_index = (length - offset) % length
    return lax.dynamic_slice_in_dim(doubled, first_index, length, axis_number)


def expand_coef(values):
    return values[:, None, :, None, None]


def body(start, energies, sites, potential):
    grid_size = potential.shape[0]
    volume = grid_size * grid_size * grid_size
    atom_count, core_count, pol_count, band_local, kpoint_local = start.shape
    plane_count = grid_size // lax.axis_size(GRID)
    position = lax.axis_index(GRID)
    chain_count = core_count * pol_count * band_local
    field_count = atom_count * chain_count
    total_count = core_count * band_local * lax.axis_size(BAND) * kpoint_local * lax.axis_size(GRID)
    cas_grid = cas_table(grid_size)
    shifted = shift_axis(potential, sites[0, 0], 0)
    shifted = shift_axis(shifted, sites[1, 0], 1)
    shifted = shift_axis(shifted, sites[2, 0], 2)
    tables = [shifted]
    shifted_all = jnp.stack(tables, axis=-1)
    slab_table = lax.dynamic_slice_in_dim(shifted_all, position * plane_count, plane_count, 1)

    def moment(left, right):
        return jnp.sum(left * right, axis=(1, 3, 4)) / total_count

    start_sum = one_axis_at_a_time(moment(start, start), GRID_BAND)
    lanczos = start / expand_coef(jnp.sqrt(start_sum))
    previous = jnp.zeros_like(start)
    beta_prev = jnp.zeros((atom_count, pol_count), jnp.float32)
    alpha_list = []
    beta_list = []
    for iteration in range(ITERS):
        spread_fields = lanczos.reshape(atom_count, chain_count, plane_count, grid_size, grid_size)
        spread_over_z = jnp.einsum(
            "arpyz,wz->pywar", spread_fields, cas_grid, precision=precise_mode
        )
        spread_over_y = jnp.einsum(
            "pywar,uy->puwar", spread_over_z, cas_grid, precision=precise_mode
        )
        direct_spectrum = lax.all_to_all(
            spread_over_y.reshape(plane_count, grid_size, grid_size, field_count),
            GRID,
            split_axis=1,
            concat_axis=0,
            tiled=True,
        )
        field_shape = direct_spectrum.shape
        over_x = jnp.einsum("xvwf,tx->tvwf", direct_spectrum, cas_grid, precision=precise_mode)
        split_view = over_x.reshape(
            field_shape[0], field_shape[1], field_shape[2], atom_count, chain_count
        )
        scaled = split_view * slab_table[..., None]
        back_x = jnp.einsum("tvwar,xt->xvwar", scaled, cas_grid, precision=precise_mode)
        weighted = back_x.reshape(field_shape)
        direct_returned = lax.all_to_all(weighted, GRID, split_axis=0, concat_axis=1, tiled=True)
        fields = direct_returned.reshape(plane_count, grid_size, grid_size, atom_count, chain_count)
        over_z = jnp.einsum("pvwar,zw->pvzar", fields, cas_grid, precision=precise_mode)
        over_y = jnp.einsum("pvzar,yv->arpyz", over_z, cas_grid, precision=precise_mode)
        applied = energies[None, :, None] * lanczos - over_y.reshape(start.shape) / volume
        moments_all = (
            one_axis_at_a_time(moment(lanczos, applied), GRID_BAND),
            one_axis_at_a_time(moment(applied, applied), GRID_BAND),
            one_axis_at_a_time(moment(lanczos, lanczos), GRID_BAND),
            one_axis_at_a_time(moment(previous, previous), GRID_BAND),
            one_axis_at_a_time(moment(previous, applied), GRID_BAND),
            one_axis_at_a_time(moment(lanczos, previous), GRID_BAND),
        )
        alpha_now = moments_all[0]
        square = (
            moments_all[1]
            + alpha_now * alpha_now * moments_all[2]
            + beta_prev * beta_prev * moments_all[3]
        )
        square = square - 2.0 * alpha_now * moments_all[0] - 2.0 * beta_prev * moments_all[4]
        square = square + 2.0 * alpha_now * beta_prev * moments_all[5]
        beta_now = jnp.sqrt(square)
        remainder = applied - expand_coef(alpha_now) * lanczos - expand_coef(beta_prev) * previous
        previous = lanczos
        lanczos = remainder / expand_coef(beta_now)
        beta_prev = beta_now
        alpha_list.append(alpha_now)
        beta_list.append(beta_now)
    return (jnp.stack(alpha_list, axis=2), jnp.stack(beta_list, axis=2), lanczos)


def solution(mesh):
    split = Mesh(mesh.devices.reshape(8, 4, 8, 2), ("grid_0", "grid_1", "band_0", "band_1"))
    placed = (P(None, None, None, BAND, GRID), P(None, BAND, GRID), P(), P())
    return jax.shard_map(
        body,
        mesh=split,
        in_specs=placed,
        out_specs=(P(), P(), P(None, None, None, BAND, GRID)),
        check_vma=False,
    )
```

profile of v0, /device:TPU:1, one launch (start us, length us, event | category | flops | bytes accessed | tf_op | source)
XLA Modules:
  0.0 446.5 jit_solution(14919644235281792380)
XLA Ops:
  2.8 15.8 %psum.652 = f32[1,1]{1,0:T(1,128)} all-reduce(f32[1,1]{1,0:T(1,128)} %bitcast), channel_id=1, replica_groups=mesh['grid_0'=8,'grid_1'=4,'band_0'=8,'band_1'=2] {'grid_0'}, use_global_device_ids=true, to_apply=%region_1.2 | all-reduce | flops 1 | bytes 8 | tf_op jit(solution)/shard_map/psum | solution.py:20
  18.6 9.1 %psum.653 = f32[1,1]{1,0:T(1,128)} all-reduce(f32[1,1]{1,0:T(1,128)} %psum.652), channel_id=1, replica_groups=mesh['grid_0'=8,'grid_1'=4,'band_0'=8,'band_1'=2] {'grid_1'}, use_global_device_ids=true, to_apply=%region_2.3 | all-reduce | flops 1 | bytes 8 | tf_op jit(solution)/shard_map/psum | solution.py:20
  27.7 20.0 %psum.654 = f32[1,1]{1,0:T(1,128)} all-reduce(f32[1,1]{1,0:T(1,128)} %psum.653), channel_id=1, replica_groups=mesh['grid_0'=8,'grid_1'=4,'band_0'=8,'band_1'=2] {'band_0'}, use_global_device_ids=true, to_apply=%region_3.4 | all-reduce | flops 1 | bytes 8 | tf_op jit(solution)/shard_map/psum | solution.py:20
  47.8 12.9 %psum.655 = f32[1,1]{1,0:T(1,128)} all-reduce(f32[1,1]{1,0:T(1,128)} %psum.654), channel_id=1, replica_groups=mesh['grid_0'=8,'grid_1'=4,'band_0'=8,'band_1'=2] {'band_1'}, use_global_device_ids=true, to_apply=%region_4.5 | all-reduce | flops 1 | bytes 8 | tf_op jit(solution)/shard_map/psum | solution.py:20
  65.2 4.8 %all-to-all-start = ((f32[32,1,512]{2,1,0:T(1,128)}), f32[32,1,512]{2,1,0:T(1,128)S(1)}, u32[]{:S(2)}, u32[]{:S(2)}) async-start(f32[32,1,512]{2,1,0:T(1,128)} %reshape.373), calls=%async_computation | async-start | bytes 131072 | tf_op jit(solution)/shard_map/all_to_all | solution.py:75
  73.2 5.6 %all-to-all-done = f32[32,1,512]{2,1,0:T(1,128)S(1)} async-done(((f32[32,1,512]{2,1,0:T(1,128)}), f32[32,1,512]{2,1,0:T(1,128)S(1)}, u32[]{:S(2)}, u32[]{:S(2)}) %all-to-all-start) | async-done | bytes 65568 | tf_op jit(solution)/shard_map/all_to_all | solution.py:75
  81.6 12.2 %all_to_all.32 = f32[32,1,512]{2,1,0:T(1,128)S(1)} all-to-all(f32[32,1,512]{2,1,0:T(1,128)S(1)} %reshape.375), channel_id=1, replica_groups=mesh['grid_0'=8,'grid_1'=4,'band_0'=8,'band_1'=2] {'grid_0','grid_1'}, dimensions={0} | all-to-all | bytes 131072 | tf_op jit(solution)/shard_map/all_to_all | solution.py:90
  102.0 15.3 %all-reduce.7 = (f32[1,1]{1,0:T(1,128)}, f32[1,1]{1,0:T(1,128)}, f32[1,1]{1,0:T(1,128)}, f32[1,1]{1,0:T(1,128)}, f32[1,1]{1,0:T(1,128)}, /*index=5*/f32[1,1]{1,0:T(1,128)}) all-reduce(f32[1,1]{1,0:T(1,128)} %bitcast.24, f32[1,1]{1,0:T(1,128)} %bitcast.21, ...), channel_id=1, replica_groups=mesh['grid_0'=8,'grid_1'=4,'band_0'=8,'band_1'=2] {'grid_0'}, use_global_device_ids=true, to_apply=%region_11.12 | all-reduce | flops 6 | bytes 48 | tf_op jit(solution)/shard_map/psum | solution.py:20
  117.3 7.8 %all-reduce.11 = (f32[1,1]{1,0:T(1,128)}, f32[1,1]{1,0:T(1,128)}, f32[1,1]{1,0:T(1,128)}, f32[1,1]{1,0:T(1,128)}, f32[1,1]{1,0:T(1,128)}, /*index=5*/f32[1,1]{1,0:T(1,128)}) all-reduce(f32[1,1]{1,0:T(1,128)} %get-tuple-element.59, ...), channel_id=1, replica_groups=mesh['grid_0'=8,'grid_1'=4,'band_0'=8,'band_1'=2] {'grid_1'}, use_global_device_ids=true, to_apply=%region_12.13 | all-reduce | flops 6 | bytes 48 | tf_op jit(solution)/shard_map/psum | solution.py:20
  125.0 11.4 %all-reduce.3 = (f32[1,1]{1,0:T(1,128)}, f32[1,1]{1,0:T(1,128)}, f32[1,1]{1,0:T(1,128)}, f32[1,1]{1,0:T(1,128)}, f32[1,1]{1,0:T(1,128)}, /*index=5*/f32[1,1]{1,0:T(1,128)}) all-reduce(f32[1,1]{1,0:T(1,128)} %get-tuple-element.80, ...), channel_id=1, replica_groups=mesh['grid_0'=8,'grid_1'=4,'band_0'=8,'band_1'=2] {'band_0'}, use_global_device_ids=true, to_apply=%region_13.14 | all-reduce | flops 6 | bytes 48 | tf_op jit(solution)/shard_map/psum | solution.py:20
  136.4 14.4 %all-reduce.15 = (f32[1,1]{1,0:T(1,128)}, f32[1,1]{1,0:T(1,128)}, f32[1,1]{1,0:T(1,128)}, f32[1,1]{1,0:T(1,128)}, f32[1,1]{1,0:T(1,128)}, /*index=5*/f32[1,1]{1,0:T(1,128)}) all-reduce(f32[1,1]{1,0:T(1,128)} %get-tuple-element.38, ...), channel_id=1, replica_groups=mesh['grid_0'=8,'grid_1'=4,'band_0'=8,'band_1'=2] {'band_1'}, use_global_device_ids=true, to_apply=%region_14.15 | all-reduce | flops 6 | bytes 48 | tf_op jit(solution)/shard_map/psum | solution.py:20
  161.2 13.1 %all_to_all.33 = f32[32,1,512]{2,1,0:T(1,128)S(1)} all-to-all(f32[32,1,512]{2,1,0:T(1,128)S(1)} %reshape.377), channel_id=1, replica_groups=mesh['grid_0'=8,'grid_1'=4,'band_0'=8,'band_1'=2] {'grid_0','grid_1'}, dimensions={0} | all-to-all | bytes 131072 | tf_op jit(solution)/shard_map/all_to_all | solution.py:75
  177.1 4.0 all-to-all-start.3
  181.8 8.2 %all-to-all-done.3 = f32[32,1,512]{2,1,0:T(1,128)S(1)} async-done(((f32[32,1,512]{2,1,0:T(1,128)}), f32[32,1,512]{2,1,0:T(1,128)S(1)}, u32[]{:S(2)}, u32[]{:S(2)}) %all-to-all-start.3) | async-done | bytes 65568 | tf_op jit(solution)/shard_map/all_to_all | solution.py:90
  197.5 14.6 %all-reduce.6 = (f32[1,1]{1,0:T(1,128)}, f32[1,1]{1,0:T(1,128)}, f32[1,1]{1,0:T(1,128)}, f32[1,1]{1,0:T(1,128)}, f32[1,1]{1,0:T(1,128)}) all-reduce(f32[1,1]{1,0:T(1,128)} %bitcast.45, f32[1,1]{1,0:T(1,128)} %bitcast.42, f32[1,1]{1,0:T(1,128)} %bitcast.46, ...), channel_id=1, replica_groups=mesh['grid_0'=8,'grid_1'=4,'band_0'=8,'band_1'=2] {'grid_0'}, use_global_device_ids=true, to_apply=%region_40.41 | all-reduce | flops 5 | bytes 40 | tf_op jit(solution)/shard_map/psum | solution.py:20
  212.2 7.5 %all-reduce.10 = (f32[1,1]{1,0:T(1,128)}, f32[1,1]{1,0:T(1,128)}, f32[1,1]{1,0:T(1,128)}, f32[1,1]{1,0:T(1,128)}, f32[1,1]{1,0:T(1,128)}) all-reduce(f32[1,1]{1,0:T(1,128)} %get-tuple-element.54, f32[1,1]{1,0:T(1,128)} %get-tuple-element.55, ...), channel_id=1, replica_groups=mesh['grid_0'=8,'grid_1'=4,'band_0'=8,'band_1'=2] {'grid_1'}, use_global_device_ids=true, to_apply=%region_41.42 | all-reduce | flops 5 | bytes 40 | tf_op jit(solution)/shard_map/psum | solution.py:20
  219.7 13.1 %all-reduce.2 = (f32[1,1]{1,0:T(1,128)}, f32[1,1]{1,0:T(1,128)}, f32[1,1]{1,0:T(1,128)}, f32[1,1]{1,0:T(1,128)}, f32[1,1]{1,0:T(1,128)}) all-reduce(f32[1,1]{1,0:T(1,128)} %get-tuple-element.75, f32[1,1]{1,0:T(1,128)} %get-tuple-element.76, ...), channel_id=1, replica_groups=mesh['grid_0'=8,'grid_1'=4,'band_0'=8,'band_1'=2] {'band_0'}, use_global_device_ids=true, to_apply=%region_42.43 | all-reduce | flops 5 | bytes 40 | tf_op jit(solution)/shard_map/psum | solution.py:20
  232.8 15.3 %all-reduce.14 = (f32[1,1]{1,0:T(1,128)}, f32[1,1]{1,0:T(1,128)}, f32[1,1]{1,0:T(1,128)}, f32[1,1]{1,0:T(1,128)}, f32[1,1]{1,0:T(1,128)}) all-reduce(f32[1,1]{1,0:T(1,128)} %get-tuple-element.33, f32[1,1]{1,0:T(1,128)} %get-tuple-element.34, ...), channel_id=1, replica_groups=mesh['grid_0'=8,'grid_1'=4,'band_0'=8,'band_1'=2] {'band_1'}, use_global_device_ids=true, to_apply=%region_43.44 | all-reduce | flops 5 | bytes 40 | tf_op jit(solution)/shard_map/psum | solution.py:20
  256.9 13.0 %all_to_all.34 = f32[32,1,512]{2,1,0:T(1,128)S(1)} all-to-all(f32[32,1,512]{2,1,0:T(1,128)S(1)} %reshape.381), channel_id=1, replica_groups=mesh['grid_0'=8,'grid_1'=4,'band_0'=8,'band_1'=2] {'grid_0','grid_1'}, dimensions={0} | all-to-all | bytes 131072 | tf_op jit(solution)/shard_map/all_to_all | solution.py:75
  272.8 3.9 all-to-all-start.5
  277.3 8.3 %all-to-all-done.5 = f32[32,1,512]{2,1,0:T(1,128)S(1)} async-done(((f32[32,1,512]{2,1,0:T(1,128)}), f32[32,1,512]{2,1,0:T(1,128)S(1)}, u32[]{:S(2)}, u32[]{:S(2)}) %all-to-all-start.5) | async-done | bytes 65568 | tf_op jit(solution)/shard_map/all_to_all | solution.py:90
  293.3 14.6 %all-reduce.5 = (f32[1,1]{1,0:T(1,128)}, f32[1,1]{1,0:T(1,128)}, f32[1,1]{1,0:T(1,128)}, f32[1,1]{1,0:T(1,128)}, f32[1,1]{1,0:T(1,128)}) all-reduce(f32[1,1]{1,0:T(1,128)} %bitcast.66, f32[1,1]{1,0:T(1,128)} %bitcast.63, f32[1,1]{1,0:T(1,128)} %bitcast.67, ...), channel_id=1, replica_groups=mesh['grid_0'=8,'grid_1'=4,'band_0'=8,'band_1'=2] {'grid_0'}, use_global_device_ids=true, to_apply=%region_65.66 | all-reduce | flops 5 | bytes 40 | tf_op jit(solution)/shard_map/psum | solution.py:20
  307.9 7.5 %all-reduce.9 = (f32[1,1]{1,0:T(1,128)}, f32[1,1]{1,0:T(1,128)}, f32[1,1]{1,0:T(1,128)}, f32[1,1]{1,0:T(1,128)}, f32[1,1]{1,0:T(1,128)}) all-reduce(f32[1,1]{1,0:T(1,128)} %get-tuple-element.49, f32[1,1]{1,0:T(1,128)} %get-tuple-element.50, ...), channel_id=1, replica_groups=mesh['grid_0'=8,'grid_1'=4,'band_0'=8,'band_1'=2] {'grid_1'}, use_global_device_ids=true, to_apply=%region_66.67 | all-reduce | flops 5 | bytes 40 | tf_op jit(solution)/shard_map/psum | solution.py:20
  315.4 11.4 %all-reduce.1 = (f32[1,1]{1,0:T(1,128)}, f32[1,1]{1,0:T(1,128)}, f32[1,1]{1,0:T(1,128)}, f32[1,1]{1,0:T(1,128)}, f32[1,1]{1,0:T(1,128)}) all-reduce(f32[1,1]{1,0:T(1,128)} %get-tuple-element.70, f32[1,1]{1,0:T(1,128)} %get-tuple-element.71, ...), channel_id=1, replica_groups=mesh['grid_0'=8,'grid_1'=4,'band_0'=8,'band_1'=2] {'band_0'}, use_global_device_ids=true, to_apply=%region_67.68 | all-reduce | flops 5 | bytes 40 | tf_op jit(solution)/shard_map/psum | solution.py:20
  326.8 15.0 %all-reduce.13 = (f32[1,1]{1,0:T(1,128)}, f32[1,1]{1,0:T(1,128)}, f32[1,1]{1,0:T(1,128)}, f32[1,1]{1,0:T(1,128)}, f32[1,1]{1,0:T(1,128)}) all-reduce(f32[1,1]{1,0:T(1,128)} %get-tuple-element.28, f32[1,1]{1,0:T(1,128)} %get-tuple-element.29, ...), channel_id=1, replica_groups=mesh['grid_0'=8,'grid_1'=4,'band_0'=8,'band_1'=2] {'band_1'}, use_global_device_ids=true, to_apply=%region_68.69 | all-reduce | flops 5 | bytes 40 | tf_op jit(solution)/shard_map/psum | solution.py:20
  350.5 13.0 %all_to_all.35 = f32[32,1,512]{2,1,0:T(1,128)S(1)} all-to-all(f32[32,1,512]{2,1,0:T(1,128)S(1)} %reshape.385), channel_id=1, replica_groups=mesh['grid_0'=8,'grid_1'=4,'band_0'=8,'band_1'=2] {'grid_0','grid_1'}, dimensions={0} | all-to-all | bytes 131072 | tf_op jit(solution)/shard_map/all_to_all | solution.py:75
  366.3 3.9 all-to-all-start.7
  370.8 8.4 %all-to-all-done.7 = f32[32,1,512]{2,1,0:T(1,128)S(1)} async-done(((f32[32,1,512]{2,1,0:T(1,128)}), f32[32,1,512]{2,1,0:T(1,128)S(1)}, u32[]{:S(2)}, u32[]{:S(2)}) %all-to-all-start.7) | async-done | bytes 65568 | tf_op jit(solution)/shard_map/all_to_all | solution.py:90
  386.9 14.6 %all-reduce.4 = (f32[1,1]{1,0:T(1,128)}, f32[1,1]{1,0:T(1,128)}, f32[1,1]{1,0:T(1,128)}, f32[1,1]{1,0:T(1,128)}, f32[1,1]{1,0:T(1,128)}) all-reduce(f32[1,1]{1,0:T(1,128)} %bitcast.84, f32[1,1]{1,0:T(1,128)} %bitcast.89, f32[1,1]{1,0:T(1,128)} %bitcast.90, ...), channel_id=1, replica_groups=mesh['grid_0'=8,'grid_1'=4,'band_0'=8,'band_1'=2] {'grid_0'}, use_global_device_ids=true, to_apply=%region_85.86 | all-reduce | flops 5 | bytes 40 | tf_op jit(solution)/shard_map/psum | solution.py:20
  401.5 7.5 %all-reduce.8 = (f32[1,1]{1,0:T(1,128)}, f32[1,1]{1,0:T(1,128)}, f32[1,1]{1,0:T(1,128)}, f32[1,1]{1,0:T(1,128)}, f32[1,1]{1,0:T(1,128)}) all-reduce(f32[1,1]{1,0:T(1,128)} %get-tuple-element.44, f32[1,1]{1,0:T(1,128)} %get-tuple-element.45, ...), channel_id=1, replica_groups=mesh['grid_0'=8,'grid_1'=4,'band_0'=8,'band_1'=2] {'grid_1'}, use_global_device_ids=true, to_apply=%region_86.87 | all-reduce | flops 5 | bytes 40 | tf_op jit(solution)/shard_map/psum | solution.py:20
  409.0 13.1 %all-reduce = (f32[1,1]{1,0:T(1,128)}, f32[1,1]{1,0:T(1,128)}, f32[1,1]{1,0:T(1,128)}, f32[1,1]{1,0:T(1,128)}, f32[1,1]{1,0:T(1,128)}) all-reduce(f32[1,1]{1,0:T(1,128)} %get-tuple-element.65, f32[1,1]{1,0:T(1,128)} %get-tuple-element.66, ...), channel_id=1, replica_groups=mesh['grid_0'=8,'grid_1'=4,'band_0'=8,'band_1'=2] {'band_0'}, use_global_device_ids=true, to_apply=%region_87.88 | all-reduce | flops 5 | bytes 40 | tf_op jit(solution)/shard_map/psum | solution.py:20
  422.1 15.2 %all-reduce.12 = (f32[1,1]{1,0:T(1,128)}, f32[1,1]{1,0:T(1,128)}, f32[1,1]{1,0:T(1,128)}, f32[1,1]{1,0:T(1,128)}, f32[1,1]{1,0:T(1,128)}) all-reduce(f32[1,1]{1,0:T(1,128)} %get-tuple-element.23, f32[1,1]{1,0:T(1,128)} %get-tuple-element.24, ...), channel_id=1, replica_groups=mesh['grid_0'=8,'grid_1'=4,'band_0'=8,'band_1'=2] {'band_1'}, use_global_device_ids=true, to_apply=%region_88.89 | all-reduce | flops 5 | bytes 40 | tf_op jit(solution)/shard_map/psum | solution.py:20
  (92 shorter events, 51.6 us)
Async XLA Ops:
  0.6 60.8 %copy-start = (f32[1,4,1,4,1024]{4,3,2,1,0:T(4,128)S(1)}, f32[1,4,1,4,1024]{4,3,2,1,0:T(4,128)}, u32[]{:S(2)}) copy-start(f32[1,4,1,4,1024]{4,3,2,1,0:T(4,128)} %param.4) | copy-start | bytes 196612
  64.2 7.8 %copy-start.2 = (f32[32,32,32]{2,1,0:T(8,128)S(1)}, f32[32,32,32]{2,1,0:T(8,128)}, u32[]{:S(2)}) copy-start(f32[32,32,32]{2,1,0:T(8,128)} %param.7) | copy-start | bytes 393220
  65.1 4.9 %copy-start.3 = (s32[3,1]{0,1:T(1,128)S(1)}, s32[3,1]{0,1:T(1,128)}, u32[]{:S(2)}) copy-start(s32[3,1]{0,1:T(1,128)} %param.6) | copy-start | bytes 40
  65.2 13.7 %all-to-all-start = ((f32[32,1,512]{2,1,0:T(1,128)}), f32[32,1,512]{2,1,0:T(1,128)S(1)}, u32[]{:S(2)}, u32[]{:S(2)}) async-start(f32[32,1,512]{2,1,0:T(1,128)} %reshape.373), calls=%async_computation | async-start | bytes 131072 | tf_op jit(solution)/shard_map/all_to_all | solution.py:75
  97.4 0.8 copy-start.1
  177.1 12.8 %all-to-all-start.3 = ((f32[32,1,512]{2,1,0:T(1,128)}), f32[32,1,512]{2,1,0:T(1,128)S(1)}, u32[]{:S(2)}, u32[]{:S(2)}) async-start(f32[32,1,512]{2,1,0:T(1,128)} %reshape.379), calls=%async_computation.3 | async-start | bytes 131072 | tf_op jit(solution)/shard_map/all_to_all | solution.py:90
  272.8 12.8 %all-to-all-start.5 = ((f32[32,1,512]{2,1,0:T(1,128)}), f32[32,1,512]{2,1,0:T(1,128)S(1)}, u32[]{:S(2)}, u32[]{:S(2)}) async-start(f32[32,1,512]{2,1,0:T(1,128)} %reshape.383), calls=%async_computation.5 | async-start | bytes 131072 | tf_op jit(solution)/shard_map/all_to_all | solution.py:90
  366.3 12.8 %all-to-all-start.7 = ((f32[32,1,512]{2,1,0:T(1,128)}), f32[32,1,512]{2,1,0:T(1,128)S(1)}, u32[]{:S(2)}, u32[]{:S(2)}) async-start(f32[32,1,512]{2,1,0:T(1,128)} %reshape.387), calls=%async_computation.7 | async-start | bytes 131072 | tf_op jit(solution)/shard_map/all_to_all | solution.py:90
where the time goes:
time: 448 us; the launch traced here: 447 us
  blocking collectives  307 us (69%)
  between operations  40.5 us (9%)
  waiting for transfers between devices  30.5 us (7%)
  matrix products  24.7 us (6%)
  other arithmetic  17.8 us (4%)
  starting transfers between devices  16.6 us (4%)
  local copies, waits for them, and re-layouts  9.11 us (2%)
    psum x20, blocking collectives, one_axis_at_a_time(): return functools.reduce(lax.psum, axes, x)  256 us
    all_to_all x3, blocking collectives, body(): lax.all_to_all(spread_over_y.reshape(plane_count, grid_size, grid_size, f...  39 us
    all_to_all x3, waiting for transfers between devices, body(): lax.all_to_all(weighted, GRID, split_axis=0, concat_axis=1, tiled=True)  24.8 us
    all_to_all x1, blocking collectives, body(): lax.all_to_all(weighted, GRID, split_axis=0, concat_axis=1, tiled=True)  12.2 us
    all_to_all x3, starting transfers between devices, body(): lax.all_to_all(weighted, GRID, split_axis=0, concat_axis=1, tiled=True)  11.7 us
  transfers between devices with their start and end apart: 4, of which 4 were waited for; matrix products, arithmetic and copies ran while one was open for 0% of the time, Pallas kernels for 0%

commit v1 on v0

v1 whole, which is shorter than its diff:
```python
import functools
import math

import jax
import jax.numpy as jnp
import numpy as np
from jax import lax
from jax.experimental import pallas as pl
from jax.experimental.pallas import tpu as pltpu
from jax.sharding import PartitionSpec as P

ITERS = 4
GRIDN = 32
ROWS = GRIDN * GRIDN * GRIDN // 128
MESH = pl.DeviceIdType.MESH
F32 = jnp.float32
BF16 = jnp.bfloat16


def cas(angle):
    return np.cos(angle) + np.sin(angle)


def halves(table):
    table = jnp.asarray(table, F32)
    high = table.astype(BF16)
    return jnp.stack([high, (table - high.astype(F32)).astype(BF16)])


def tables():
    n, eight, four = np.arange(32), np.arange(8), np.arange(4)
    along = cas(2 * math.pi * np.outer(n, n) / 32)
    plus = cas(2 * math.pi * np.outer(eight, eight) / 8)
    minus = cas(-2 * math.pi * np.outer(eight, eight) / 8)
    left = np.concatenate([np.kron(along, plus), np.kron(along, minus)], axis=0)
    turn = 2 * math.pi * np.outer(four, four) / 4
    right = np.concatenate([np.kron(np.cos(turn), along), np.kron(np.sin(turn), along)], axis=0)
    angle = np.repeat(2 * math.pi * np.outer(eight, four) / 32, 32, axis=1)
    twist = np.stack([np.cos(angle), np.sin(angle)]).astype(np.float32)
    return halves(left), halves(left.T), halves(right), halves(right.T), jnp.asarray(twist)


def cut(x):
    high = x.astype(BF16)
    return high, (x - high.astype(F32)).astype(BF16)


def mm(a, b):
    return jnp.dot(a, b, preferred_element_type=F32)


def left_product(table, x):
    high, low = cut(x)
    wide = mm(table[0], jnp.concatenate([high, low], axis=1))
    return wide[:, :128] + wide[:, 128:] + mm(table[1], high)


def right_product(x, table):
    high, low = cut(x)
    return mm(high, table[0]) + mm(low, table[0]) + mm(high, table[1])


def to_spectrum(x, left, right, cosine, sine):
    both = left_product(left, x)
    a, b = both[:ROWS], both[ROWS:]
    return right_product(jnp.concatenate([cosine * a + sine * b, cosine * b - sine * a], axis=1), right)


def from_spectrum(x, left_t, right_t, cosine, sine):
    both = right_product(x, right_t)
    a, b = both[:, :128], both[:, 128:]
    return left_product(left_t, jnp.concatenate([cosine * a - sine * b, sine * a + cosine * b], axis=0))


def total(x):
    return jnp.sum(x, axis=(0, 1), keepdims=True)


def inverse(x):
    return jnp.where(x > 0.0, 1.0 / jnp.where(x > 0.0, x, 1.0), 0.0)


def kernel(
    size,
    start_ref,
    energy_ref,
    sites_ref,
    potential_ref,
    left_ref,
    left_t_ref,
    right_ref,
    right_t_ref,
    twist_ref,
    out_ref,
    alpha_ref,
    beta_ref,
    field_buf,
    energy_buf,
    doubled,
    weight_buf,
    krylov,
    basis,
    line_buf,
    plane_buf,
    field_send,
    field_recv,
    energy_send,
    energy_recv,
    basis_send,
    basis_recv,
    line_send,
    line_recv,
    plane_send,
    plane_recv,
):
    grids, bands, fields, planes, inner_total = size
    layers = bands // 2
    ratio = grids // fields
    me = lax.axis_index("grid")
    band = lax.axis_index("band")
    core = lax.rem(band, 2)
    layer = lax.div(band, 2)
    partner = band + 1 - 2 * core
    mine = lax.div(me, ratio)
    lag = lax.rem(core, ratio)
    computes = lax.rem(me, ratio) == lag
    slot = core * fields + mine

    def copy(src, dst, send, recv, grid_to, band_to):
        return pltpu.make_async_remote_copy(
            src_ref=src,
            dst_ref=dst,
            send_sem=send,
            recv_sem=recv,
            device_id={"grid": grid_to, "band": band_to},
            device_id_type=MESH,
        )

    def here(ref, send, recv):
        return copy(ref, ref, send, recv, me, band)

    barrier = pltpu.get_barrier_semaphore()

    def greet(grid_to, band_to):
        pl.semaphore_signal(
            barrier, inc=1, device_id={"grid": grid_to, "band": band_to}, device_id_type=MESH
        )

    @pl.loop(1, grids)
    def _(i):
        greet(lax.rem(me + i, grids), band)

    @pl.loop(0, grids)
    def _(i):
        greet(lax.rem(me + i, grids), partner)

    @pl.loop(1, layers)
    def _(i):
        greet(me, lax.rem(band + 2 * i, bands))

    @pl.when(computes)
    def _():
        sx, sy, sz = sites_ref[0, 0], sites_ref[1, 0], sites_ref[2, 0]
        doubled[:, 0:GRIDN, :] = potential_ref[...]
        doubled[:, GRIDN : 2 * GRIDN, :] = potential_ref[...]
        from_z = lax.broadcasted_iota(jnp.int32, (GRIDN, 128), 0)
        to_z = lax.broadcasted_iota(jnp.int32, (GRIDN, 128), 1)
        weights = jnp.zeros((ROWS, 128), F32)
        for v1 in range(4):
            first = lax.rem(8 * v1 - sy + GRIDN, GRIDN)
            rows = jnp.concatenate(
                [doubled[lax.rem(x - sx + GRIDN, GRIDN), pl.ds(first, 8), :] for x in range(GRIDN)], axis=0
            )
            lands = lax.rem(from_z + sz, GRIDN) + GRIDN * v1
            choose = jnp.where(lands == to_z, 1.0, 0.0).astype(BF16)
            high = rows.astype(BF16)
            rest = rows - high.astype(F32)
            middle = rest.astype(BF16)
            low = (rest - middle.astype(F32)).astype(BF16)
            weights = weights + (mm(high, choose) + mm(middle, choose) + mm(low, choose))
        weight_buf[...] = weights * (1.0 / (GRIDN * GRIDN * GRIDN))

    pl.semaphore_wait(barrier, 2 * grids - 1 + layers - 1)

    for src, dst, send, recv in (
        (start_ref, field_buf, field_send, field_recv),
        (energy_ref, energy_buf, energy_send, energy_recv),
    ):

        @pl.loop(1, fields)
        def _(i, src=src, dst=dst, send=send, recv=recv):
            field = lax.rem(mine + i, fields)
            copy(src.at[field], dst.at[pl.ds(me * planes, planes)], send, recv, field * ratio + lag, band).start()

        @pl.when(jnp.logical_not(computes))
        def _(src=src, dst=dst, send=send, recv=recv):
            copy(src.at[mine], dst.at[pl.ds(me * planes, planes)], send, recv, mine * ratio + lag, band).start()

        @pl.when(computes)
        def _(src=src, dst=dst):
            dst[pl.ds(me * planes, planes)] = src[mine]

    @pl.when(computes)
    def _():
        left, left_t, right, right_t = left_ref, left_t_ref, right_ref, right_t_ref
        cosine = jnp.concatenate([twist_ref[0]] * (ROWS // 8), axis=0)
        sine = jnp.concatenate([twist_ref[1]] * (ROWS // 8), axis=0)
        rest = pl.ds(0, (grids - 1) * planes)
        here(field_buf.at[rest], field_send, field_recv).wait_recv()
        vector = field_buf[...].reshape(ROWS, 128)
        square = total(vector * vector)
        now = vector * inverse(jnp.sqrt(square))
        before = None
        beta = None
        record = [square]
        betas = []
        for step in range(ITERS):
            spectrum = to_spectrum(now, left, right, cosine, sine)
            direct = from_spectrum(spectrum * weight_buf[...], left_t, right_t, cosine, sine)
            if step == 0:
                here(energy_buf.at[rest], energy_send, energy_recv).wait_recv()
            applied = energy_buf[...].reshape(ROWS, 128) * now - direct
            alpha = total(now * applied)
            remainder = applied - alpha * now
            if step:
                remainder = remainder - beta * before
            beta = jnp.sqrt(total(remainder * remainder))
            before = now
            now = remainder * inverse(beta)
            record.append(alpha)
            betas.append(beta)
            krylov[step] = now.reshape(GRIDN, 8, 128)

            @pl.loop(1, grids)
            def _(i, step=step):
                to = lax.rem(me + i, grids)
                copy(
                    krylov.at[step, pl.ds(to * planes, planes)],
                    basis.at[mine, step],
                    basis_send,
                    basis_recv,
                    to,
                    band,
                ).start()

            basis[mine, step] = krylov[step, pl.ds(me * planes, planes)]
        lanes = lax.broadcasted_iota(jnp.int32, (1, 128), 1)
        row = jnp.zeros((1, 128), F32)
        for k, value in enumerate(record + betas):
            row = jnp.where(lanes == 16 * layer + k, value, row)
        line_buf[layer] = row

        @pl.loop(1, layers)
        def _(i):
            copy(line_buf.at[layer], line_buf.at[layer], line_send, line_recv, me, lax.rem(band + 2 * i, bands)).start()

        here(line_buf.at[pl.ds(0, layers - 1)], line_send, line_recv).wait_recv()
        plane_buf[slot] = jnp.sum(line_buf[...], axis=0)

        @pl.loop(1, grids)
        def _(i):
            copy(plane_buf.at[slot], plane_buf.at[slot], plane_send, plane_recv, lax.rem(me + i, grids), band).start()

        @pl.loop(0, grids)
        def _(i):
            copy(plane_buf.at[slot], plane_buf.at[slot], plane_send, plane_recv, lax.rem(me + i, grids), partner).start()

        here(plane_buf.at[pl.ds(0, 2 * fields - 1)], plane_send, plane_recv).wait_recv()
        here(basis.at[pl.ds(0, fields - 1)], basis_send, basis_recv).wait_recv()

    @pl.when(jnp.logical_not(computes))
    def _():
        here(plane_buf, plane_send, plane_recv).wait_recv()
        here(basis, basis_send, basis_recv).wait_recv()

    gathered = plane_buf[...].reshape(2 * fields, 128)

    def coefficient(k):
        return gathered if k == 0 else pltpu.roll(gathered, 128 - k, 1)

    lanes = lax.broadcasted_iota(jnp.int32, (2 * fields, 128), 1)
    square = jnp.where(lax.rem(lanes, 16) == 0, gathered, 0.0)
    alphas = [coefficient(1 + j) for j in range(ITERS)]
    betas = [coefficient(1 + ITERS + j) for j in range(ITERS)]
    length = jnp.sqrt(square)
    now = [length / jnp.sqrt(total(square))]
    before = []
    beta = None
    alpha_row = jnp.zeros((1, ITERS), F32)
    beta_row = jnp.zeros((1, ITERS), F32)
    place = lax.broadcasted_iota(jnp.int32, (1, ITERS), 1)
    for step in range(ITERS):
        applied = []
        for i in range(step + 2):
            terms = []
            if i < len(now):
                terms.append(alphas[i] * now[i])
            if i:
                terms.append(betas[i - 1] * now[i - 1])
            if i + 1 < len(now):
                terms.append(betas[i] * now[i + 1])
            applied.append(functools.reduce(jnp.add, terms))
        alpha = total(functools.reduce(jnp.add, [a * b for a, b in zip(now, applied)]))
        remainder = []
        for i, value in enumerate(applied):
            if i < len(now):
                value = value - alpha * now[i]
            if i < len(before):
                value = value - beta * before[i]
            remainder.append(value)
        beta = jnp.sqrt(total(functools.reduce(jnp.add, [value * value for value in remainder])))
        before = now
        now = [value / beta for value in remainder]
        alpha_row = jnp.where(place == step, alpha, alpha_row)
        beta_row = jnp.where(place == step, beta, beta_row)
    alpha_ref[0] = alpha_row
    beta_ref[0] = beta_row
    now[0] = now[0] * inverse(length)
    own = lanes[:fields] == 16 * layer
    shares = []
    for value in now:
        part = jnp.where(core == 0, value[:fields], value[fields:])
        shares.append(math.sqrt(inner_total) * jnp.sum(jnp.where(own, part, 0.0), axis=1, keepdims=True))
    for f in range(fields):
        result = start_ref[f] * shares[0][f : f + 1].reshape(1, 1, 1)
        for step in range(ITERS):
            result = result + basis[f, step] * shares[1 + step][f : f + 1].reshape(1, 1, 1)
        out_ref[f] = result

    @pl.when(computes)
    def _():
        here(start_ref.at[pl.ds(0, fields - 1)], field_send, field_recv).wait_send()
        here(energy_ref.at[pl.ds(0, fields - 1)], energy_send, energy_recv).wait_send()
        here(krylov.at[:, pl.ds(0, (grids - 1) * planes)], basis_send, basis_recv).wait_send()
        here(line_buf.at[pl.ds(0, layers - 1)], line_send, line_recv).wait_send()
        here(plane_buf.at[pl.ds(0, grids - 1)], plane_send, plane_recv).wait_send()
        here(plane_buf.at[pl.ds(0, grids)], plane_send, plane_recv).wait_send()

    @pl.when(jnp.logical_not(computes))
    def _():
        here(start_ref, field_send, field_recv).wait_send()
        here(energy_ref, energy_send, energy_recv).wait_send()


def body(size, start, energies, sites, potential):
    grids, bands, fields, planes, _ = size
    slab = (fields, planes, 8, 128)
    vmem = pl.BlockSpec(memory_space=pltpu.VMEM)
    smem = pl.BlockSpec(memory_space=pltpu.SMEM)
    dma = pltpu.SemaphoreType.DMA
    out, alphas, betas = pl.pallas_call(
        functools.partial(kernel, size),
        out_shape=(
            jax.ShapeDtypeStruct(slab, F32),
            jax.ShapeDtypeStruct((1, 1, ITERS), F32),
            jax.ShapeDtypeStruct((1, 1, ITERS), F32),
        ),
        in_specs=[vmem, vmem, smem] + [vmem] * 6,
        out_specs=(vmem, vmem, vmem),
        scratch_shapes=[
            pltpu.VMEM((GRIDN, 8, 128), F32),
            pltpu.VMEM((GRIDN, 8, 128), F32),
            pltpu.VMEM((GRIDN, 2 * GRIDN, GRIDN), F32),
            pltpu.VMEM((ROWS, 128), F32),
            pltpu.VMEM((ITERS, GRIDN, 8, 128), F32),
            pltpu.VMEM((fields, ITERS, planes, 8, 128), F32),
            pltpu.VMEM((bands // 2, 1, 128), F32),
            pltpu.VMEM((2 * fields, 1, 128), F32),
        ]
        + [dma] * 10,
        compiler_params=pltpu.CompilerParams(collective_id=0, has_side_effects=True),
    )(start.reshape(slab), energies.reshape(slab), sites, potential, *tables())
    return alphas, betas, out.reshape(start.shape)


def solution(mesh):
    grids, bands = mesh.shape["grid"], mesh.shape["band"]

    def whole(start, energies, sites, potential):
        atoms, cores, pols, band_count, points = start.shape
        fields = cores * band_count // bands
        size = (grids, bands, fields, GRIDN // grids, cores * band_count * points)
        return jax.shard_map(
            functools.partial(body, size),
            mesh=mesh,
            in_specs=(P(None, None, None, "band", "grid"), P(None, "band", "grid"), P(), P()),
            out_specs=(P(), P(), P(None, None, None, "band", "grid")),
            check_vma=False,
        )(start, energies, sites, potential)

    return whole
```

time: 448 us -> 53.2 us (0.12)
  blocking collectives: 307 us -> 0 us
  Pallas kernels: 0 us -> 45.6 us
  between operations: 40.5 us -> 0.64 us
  waiting for transfers between devices: 30.5 us -> 0 us
  matrix products: 24.7 us -> 0 us
  other arithmetic: 17.8 us -> 0 us
  starting transfers between devices: 16.6 us -> 0 us
    psum x20 -> x0, blocking collectives: 256 us -> none  [one_axis_at_a_time(): return functools.reduce(lax.psum, axes, x)]
    all_to_all x4 -> x0, blocking collectives: 51.3 us -> none  [the longest x3 39 us: body(): lax.all_to_all(spread_over_y.reshape(plane_count, grid_size, grid_size, f...]
    pallas_call x0 -> x1, Pallas kernels: none -> 45.6 us  [body(): pl.pallas_call(functools.partial(kernel, size), out_shape=(jax.ShapeDtype...]
    all_to_all x4 -> x0, waiting for transfers between devices: 30.5 us -> none  [the longest x3 24.8 us: body(): lax.all_to_all(weighted, GRID, split_axis=0, concat_axis=1, tiled=True)]
    dot_general x24 -> x0, matrix products: 24.7 us -> none  [the longest x4 5.31 us: body(): jnp.einsum('pvzar,yv->arpyz', over_z, cas_grid, precision=precise_mode)]
    all_to_all x4 -> x0, starting transfers between devices: 16.6 us -> none  [the longest x3 11.7 us: body(): lax.all_to_all(weighted, GRID, split_axis=0, concat_axis=1, tiled=True)]
    all_to_all x8 -> x0, other arithmetic: 6.39 us -> none  [the longest x4 3.19 us: body(): lax.all_to_all(weighted, GRID, split_axis=0, concat_axis=1, tiled=True)]
    reduce_sum x5 -> x0, other arithmetic: 4.55 us -> none  [moment(): return jnp.sum(left * right, axis=(1, 3, 4)) / total_count]
  transfers between devices with their start and end apart: 4 -> 0, of which waited for: 4 -> 0; matrix products, arithmetic and copies ran while one was open for 0% -> 0% of each run, Pallas kernels for 0% -> 0%
where the time goes in v1:
time: 53.2 us; the launch traced here: 52.9 us
  Pallas kernels  45.6 us (86%)
  local copies, waits for them, and re-layouts  6.71 us (13%)
  between operations  0.64 us (1%)
    pallas_call x1, Pallas kernels, body(): pl.pallas_call(functools.partial(kernel, size), out_shape=(jax.ShapeDtype...  45.6 us
    unnamed x9, local copies, waits for them, and re-layouts  3.05 us
    reshape x1, local copies, waits for them, and re-layouts, body(): start.reshape(slab)  1.53 us
    reshape x1, local copies, waits for them, and re-layouts, body(): return (alphas, betas, out.reshape(start.shape))  1.49 us

profile of v1, /device:TPU:1, one launch (start us, length us, event | category | flops | bytes accessed | tf_op | source)
XLA Modules:
  0.0 52.9 jit_solution(15162204005145569305)
XLA Ops:
  0.6 1.3 %copy.12.sites_ref = s32[3,1]{1,0:T(4,128)} copy(s32[3,1]{0,1:T(1,128)} %param.11) | data formatting | bytes 24 | tf_op args[2]
  1.9 0.0 copy-start
  1.9 1.5 %reshape.15.start_ref = f32[16,1,8,128]{3,2,1,0:T(8,128)} reshape(f32[1,4,1,4,1024]{4,3,2,1,0:T(4,128)} %param.9) | data formatting | bytes 131072 | tf_op jit(solution)/shard_map/reshape | solution.py:372
  3.5 0.0 copy-done
  3.5 0.6 %reshape.16.energy_ref = f32[16,1,8,128]{3,2,1,0:T(8,128)} reshape(f32[4,4,1024]{2,1,0:T(4,128)S(1)} %copy-done) | data formatting | bytes 131072 | tf_op jit(solution)/shard_map/reshape | solution.py:372
  4.1 45.6 %shard_map.112 = (f32[16,1,8,128]{3,2,1,0:T(8,128)}, f32[1,1,4]{2,1,0:T(1,128)}, f32[1,1,4]{2,1,0:T(1,128)}) custom-call(f32[16,1,8,128]{3,2,1,0:T(8,128)} %reshape.15.start_ref, f32[16,1,8,128]{3,2,1,0:T(8,128)} %reshape.16.energy_ref, s32[3,1]{1,0:T(4,128)} %copy.12.sites_ref, f32[32,32,32]{2,1,0:T(8,128)} %potential_ref.1, ...), custom_call_target="tpu_custom_call" | custom-call | tf_op jit(solution)/shard_map/pallas_call | solution.py:351
  49.7 1.5 %reshape.17 = f32[1,4,1,4,1024]{4,3,1,2,0:T(4,128)} reshape(f32[16,1,8,128]{3,2,1,0:T(8,128)} %get-tuple-element.8) | data formatting | bytes 131072 | tf_op jit(solution)/shard_map/reshape | solution.py:373
  51.2 0.0 copy-start.2
  51.2 0.6 %copy-done.2 = f32[1,1,4]{2,1,0:T(1,128)S(1)} copy-done((f32[1,1,4]{2,1,0:T(1,128)S(1)}, f32[1,1,4]{2,1,0:T(1,128)}, u32[]{:S(2)}) %copy-start.2) | copy-done | bytes 40
  51.8 0.0 copy-start.1
  51.8 0.5 copy.16
  52.3 0.1 copy-done.1
  52.4 0.5 copy.17
Async XLA Ops:
  1.9 1.5 %copy-start = (f32[4,4,1024]{2,1,0:T(4,128)S(1)}, f32[4,4,1024]{2,1,0:T(4,128)}, u32[]{:S(2)}) copy-start(f32[4,4,1024]{2,1,0:T(4,128)} %param.10) | copy-start | bytes 196612
  51.2 0.6 %copy-start.2 = (f32[1,1,4]{2,1,0:T(1,128)S(1)}, f32[1,1,4]{2,1,0:T(1,128)}, u32[]{:S(2)}) copy-start(f32[1,1,4]{2,1,0:T(1,128)} %get-tuple-element.15) | copy-start | bytes 52
  51.8 0.6 %copy-start.1 = (f32[1,1,4]{2,1,0:T(1,128)S(1)}, f32[1,1,4]{2,1,0:T(1,128)}, u32[]{:S(2)}) copy-start(f32[1,1,4]{2,1,0:T(1,128)} %get-tuple-element.16) | copy-start | bytes 52

commit v2 on v1

v2 whole, which is shorter than its diff:
```python
import functools
import math

import jax
import jax.numpy as jnp
import numpy as np
from jax import lax
from jax.experimental import pallas as pl
from jax.experimental.pallas import tpu as pltpu
from jax.sharding import PartitionSpec as P

ITERS = 4
GRIDN = 32
ROWS = GRIDN * GRIDN * GRIDN // 128
MESH = pl.DeviceIdType.MESH
F32 = jnp.float32
BF16 = jnp.bfloat16


def cas(angle):
    return np.cos(angle) + np.sin(angle)


def halves(table):
    table = jnp.asarray(table, F32)
    high = table.astype(BF16)
    return jnp.stack([high, (table - high.astype(F32)).astype(BF16)])


def tables():
    n, eight, four = np.arange(32), np.arange(8), np.arange(4)
    along = cas(2 * math.pi * np.outer(n, n) / 32)
    plus = cas(2 * math.pi * np.outer(eight, eight) / 8)
    minus = cas(-2 * math.pi * np.outer(eight, eight) / 8)
    left = np.concatenate([np.kron(along, plus), np.kron(along, minus)], axis=0)
    turn = 2 * math.pi * np.outer(four, four) / 4
    right = np.concatenate([np.kron(np.cos(turn), along), np.kron(np.sin(turn), along)], axis=0)
    angle = np.repeat(2 * math.pi * np.outer(eight, four) / 32, 32, axis=1)
    twist = np.stack([np.cos(angle), np.sin(angle)]).astype(np.float32)
    return halves(left), halves(left.T), halves(right), halves(right.T), jnp.asarray(twist)


def cut(x):
    high = x.astype(BF16)
    return high, (x - high.astype(F32)).astype(BF16)


def mm(a, b):
    return jnp.dot(a, b, preferred_element_type=F32)


def left_product(table, x):
    high, low = cut(x)
    wide = mm(table[0], jnp.concatenate([high, low], axis=1))
    return wide[:, :128] + wide[:, 128:] + mm(table[1], high)


def right_product(x, table):
    high, low = cut(x)
    return mm(high, table[0]) + mm(low, table[0]) + mm(high, table[1])


def to_spectrum(x, left, right, cosine, sine):
    both = left_product(left, x)
    a, b = both[:ROWS], both[ROWS:]
    return right_product(jnp.concatenate([cosine * a + sine * b, cosine * b - sine * a], axis=1), right)


def from_spectrum(x, left_t, right_t, cosine, sine):
    both = right_product(x, right_t)
    a, b = both[:, :128], both[:, 128:]
    return left_product(left_t, jnp.concatenate([cosine * a - sine * b, sine * a + cosine * b], axis=0))


def total(x):
    return jnp.sum(x, axis=(0, 1), keepdims=True)


def inverse(x):
    return jnp.where(x > 0.0, 1.0 / jnp.where(x > 0.0, x, 1.0), 0.0)


def exchange_kernel(
    size,
    start_ref,
    energy_ref,
    sites_ref,
    potential_ref,
    left_hbm,
    left_t_hbm,
    right_hbm,
    right_t_hbm,
    twist_hbm,
    plane_buf,
    basis,
    start_stage,
    energy_stage,
    sites_smem,
    left,
    left_t,
    right,
    right_t,
    twist,
    energy_out,
    field_buf,
    energy_buf,
    doubled,
    weight_buf,
    krylov,
    line_buf,
    local_sems,
    field_send,
    field_recv,
    energy_send,
    energy_recv,
    basis_send,
    basis_recv,
    line_send,
    line_recv,
    plane_send,
    plane_recv,
):
    grids, bands, fields, planes, band_local, _ = size
    layers = bands // 2
    ratio = grids // fields
    me = lax.axis_index("grid")
    band = lax.axis_index("band")
    core = lax.rem(band, 2)
    layer = lax.div(band, 2)
    partner = band + 1 - 2 * core
    mine = lax.div(me, ratio)
    lag = lax.rem(core, ratio)
    computes = lax.rem(me, ratio) == lag
    slot = core * fields + mine
    everyone = functools.partial(pl.loop, unroll=True)

    def copy(src, dst, send, recv, grid_to, band_to):
        return pltpu.make_async_remote_copy(
            src_ref=src,
            dst_ref=dst,
            send_sem=send,
            recv_sem=recv,
            device_id={"grid": grid_to, "band": band_to},
            device_id_type=MESH,
        )

    def here(ref, send, recv):
        return copy(ref, ref, send, recv, me, band)

    loads = [
        pltpu.make_async_copy(src, dst, local_sems.at[i])
        for i, (src, dst) in enumerate(
            [
                (start_ref, start_stage),
                (energy_ref, energy_stage),
                (sites_ref, sites_smem),
                (potential_ref, doubled.at[:, pl.ds(0, GRIDN), :]),
                (potential_ref, doubled.at[:, pl.ds(GRIDN, GRIDN), :]),
                (left_hbm, left),
                (right_hbm, right),
                (twist_hbm, twist),
                (left_t_hbm, left_t),
                (right_t_hbm, right_t),
            ]
        )
    ]
    loads[0].start()
    loads[1].start()
    barrier = pltpu.get_barrier_semaphore()

    def greet(grid_to, band_to):
        pl.semaphore_signal(
            barrier, inc=1, device_id={"grid": grid_to, "band": band_to}, device_id_type=MESH
        )

    @everyone(1, grids)
    def _(i):
        greet(lax.rem(me + i, grids), band)

    @everyone(0, grids)
    def _(i):
        greet(lax.rem(me + i, grids), partner)

    @everyone(1, layers)
    def _(i):
        greet(me, lax.rem(band + 2 * i, bands))

    @pl.when(computes)
    def _():
        for load in loads[2:]:
            load.start()

    loads[0].wait()
    loads[1].wait()
    for f in range(fields):
        first = f // band_local * (band_local * 8 * planes) + f % band_local
        rows = pl.ds(first, 8 * planes, stride=band_local)
        basis[f, 0] = start_stage[rows, :].reshape(planes, 8, 128)
        energy_out[f] = energy_stage[rows, :].reshape(planes, 8, 128)

    @pl.when(computes)
    def _():
        for load in loads[2:5]:
            load.wait()
        sx, sy, sz = sites_smem[0, 0], sites_smem[0, 1], sites_smem[0, 2]
        from_z = lax.broadcasted_iota(jnp.int32, (GRIDN, 128), 0)
        to_z = lax.broadcasted_iota(jnp.int32, (GRIDN, 128), 1)
        weights = jnp.zeros((ROWS, 128), F32)
        for v1 in range(4):
            first = lax.rem(8 * v1 - sy + GRIDN, GRIDN)
            rows = jnp.concatenate(
                [doubled[lax.rem(x - sx + GRIDN, GRIDN), pl.ds(first, 8), :] for x in range(GRIDN)], axis=0
            )
            lands = lax.rem(from_z + sz, GRIDN) + GRIDN * v1
            choose = jnp.where(lands == to_z, 1.0, 0.0).astype(BF16)
            high = rows.astype(BF16)
            rest = rows - high.astype(F32)
            middle = rest.astype(BF16)
            low = (rest - middle.astype(F32)).astype(BF16)
            weights = weights + (mm(high, choose) + mm(middle, choose) + mm(low, choose))
        weight_buf[...] = weights * (1.0 / (GRIDN * GRIDN * GRIDN))

    pl.semaphore_wait(barrier, 2 * grids - 1 + layers - 1)

    def source(src, f):
        return src.at[f, 0] if src is basis else src.at[f]

    for src, dst, send, recv in (
        (basis, field_buf, field_send, field_recv),
        (energy_out, energy_buf, energy_send, energy_recv),
    ):

        @everyone(1, fields)
        def _(i, src=src, dst=dst, send=send, recv=recv):
            field = lax.rem(mine + i, fields)
            copy(
                source(src, field), dst.at[pl.ds(me * planes, planes)], send, recv, field * ratio + lag, band
            ).start()

        @pl.when(jnp.logical_not(computes))
        def _(src=src, dst=dst, send=send, recv=recv):
            copy(
                source(src, mine), dst.at[pl.ds(me * planes, planes)], send, recv, mine * ratio + lag, band
            ).start()

    @pl.when(computes)
    def _():
        field_buf[pl.ds(me * planes, planes)] = basis[mine, 0]
        energy_buf[pl.ds(me * planes, planes)] = energy_out[mine]
        for load in loads[5:]:
            load.wait()
        others = pl.ds(0, (grids - 1) * planes)
        here(field_buf.at[others], field_send, field_recv).wait_recv()
        cosine = jnp.concatenate([twist[0]] * (ROWS // 8), axis=0)
        sine = jnp.concatenate([twist[1]] * (ROWS // 8), axis=0)
        rest = field_buf[...].reshape(ROWS, 128)
        now = before = beta = None
        alphas = []
        squares = []
        for step in range(ITERS):
            square = total(rest * rest)
            squares.append(square)
            spectrum = to_spectrum(rest, left, right, cosine, sine)
            direct = from_spectrum(spectrum * weight_buf[...], left_t, right_t, cosine, sine)
            length = jnp.sqrt(square)
            scale = inverse(length)
            if step == 0:
                here(energy_buf.at[others], energy_send, energy_recv).wait_recv()
            before, beta = now, length
            now = rest * scale
            applied = energy_buf[...].reshape(ROWS, 128) * now - direct * scale
            if step:
                applied = applied - beta * before
            alpha = total(now * applied)
            rest = applied - alpha * now
            alphas.append(alpha)
            krylov[step] = rest.reshape(GRIDN, 8, 128)

            @everyone(1, grids)
            def _(i, step=step):
                to = lax.rem(me + i, grids)
                copy(
                    krylov.at[step, pl.ds(to * planes, planes)],
                    basis.at[mine, 1 + step],
                    basis_send,
                    basis_recv,
                    to,
                    band,
                ).start()

            basis[mine, 1 + step] = krylov[step, pl.ds(me * planes, planes)]
        squares.append(total(rest * rest))
        lanes = lax.broadcasted_iota(jnp.int32, (1, 128), 1)
        row = jnp.zeros((1, 128), F32)
        for k, value in enumerate(squares + alphas):
            row = jnp.where(lanes == 16 * layer + k, value, row)
        line_buf[layer] = row

        @everyone(1, layers)
        def _(i):
            copy(
                line_buf.at[layer], line_buf.at[layer], line_send, line_recv, me, lax.rem(band + 2 * i, bands)
            ).start()

        here(line_buf.at[pl.ds(0, layers - 1)], line_send, line_recv).wait_recv()
        plane_buf[slot] = jnp.sum(line_buf[...], axis=0)

        @everyone(1, grids)
        def _(i):
            copy(
                plane_buf.at[slot], plane_buf.at[slot], plane_send, plane_recv, lax.rem(me + i, grids), band
            ).start()

        @everyone(0, grids)
        def _(i):
            copy(
                plane_buf.at[slot], plane_buf.at[slot], plane_send, plane_recv, lax.rem(me + i, grids), partner
            ).start()

        here(plane_buf.at[pl.ds(0, 2 * fields - 1)], plane_send, plane_recv).wait_recv()
        arrived = basis.at[pl.ds(0, fields - 1), pl.ds(1, ITERS)]
        here(arrived, basis_send, basis_recv).wait_recv()
        here(basis.at[pl.ds(0, fields - 1), 0], field_send, field_recv).wait_send()
        here(energy_out.at[pl.ds(0, fields - 1)], energy_send, energy_recv).wait_send()
        here(krylov.at[:, pl.ds(0, (grids - 1) * planes)], basis_send, basis_recv).wait_send()
        here(line_buf.at[pl.ds(0, layers - 1)], line_send, line_recv).wait_send()
        here(plane_buf.at[pl.ds(0, grids - 1)], plane_send, plane_recv).wait_send()
        here(plane_buf.at[pl.ds(0, grids)], plane_send, plane_recv).wait_send()

    @pl.when(jnp.logical_not(computes))
    def _():
        here(plane_buf, plane_send, plane_recv).wait_recv()
        here(basis.at[:, pl.ds(1, ITERS)], basis_send, basis_recv).wait_recv()
        here(basis.at[:, 0], field_send, field_recv).wait_send()
        here(energy_out, energy_send, energy_recv).wait_send()


def merge_kernel(size, plane_buf, basis, out_ref, alpha_ref, beta_ref):
    grids, bands, fields, planes, band_local, inner_total = size
    band = lax.axis_index("band")
    core = lax.rem(band, 2)
    layer = lax.div(band, 2)
    gathered = plane_buf[...].reshape(2 * fields, 128)
    lanes = lax.broadcasted_iota(jnp.int32, (2 * fields, 128), 1)
    valid = lax.rem(lanes, 16) == 0

    def coefficient(k):
        return jnp.where(valid, gathered if k == 0 else pltpu.roll(gathered, 128 - k, 1), 0.0)

    lengths = [jnp.sqrt(coefficient(k)) for k in range(ITERS + 1)]
    diagonal = [coefficient(1 + ITERS + k) for k in range(ITERS)]
    offs = lengths[1:]
    rest = [lengths[0]]
    before = []
    beta = None
    place = lax.broadcasted_iota(jnp.int32, (1, ITERS), 1)
    alpha_row = jnp.zeros((1, ITERS), F32)
    beta_row = jnp.zeros((1, ITERS), F32)
    for step in range(ITERS + 1):
        square = total(functools.reduce(jnp.add, [value * value for value in rest]))
        length = jnp.sqrt(square)
        scale = 1.0 / length
        if step:
            beta_row = jnp.where(place == step - 1, length, beta_row)
        if step == ITERS:
            rest = [value * scale for value in rest]
            break
        applied = []
        for i in range(step + 2):
            terms = []
            if i < len(rest):
                terms.append(diagonal[i] * rest[i])
            if i:
                terms.append(offs[i - 1] * rest[i - 1])
            if i + 1 < len(rest):
                terms.append(offs[i] * rest[i + 1])
            applied.append(functools.reduce(jnp.add, terms))
        alpha = total(functools.reduce(jnp.add, [a * b for a, b in zip(rest, applied)])) / square
        alpha_row = jnp.where(place == step, alpha, alpha_row)
        after = []
        for i, value in enumerate(applied):
            if i < len(rest):
                value = value - alpha * rest[i]
            value = value * scale
            if i < len(before):
                value = value - length * before[i]
            after.append(value)
        before = [value * scale for value in rest]
        rest = after
    alpha_ref[0] = alpha_row
    beta_ref[0] = beta_row
    own = lanes[:fields] == 16 * layer
    shares = []
    for value, length in zip(rest, lengths):
        value = value * inverse(length)
        part = jnp.where(core == 0, value[:fields], value[fields:])
        shares.append(math.sqrt(inner_total) * jnp.sum(jnp.where(own, part, 0.0), axis=1, keepdims=True))
    for f in range(fields):
        terms = [
            basis[f, k].reshape(8 * planes, 128) * shares[k][f : f + 1].reshape(1, 1) for k in range(ITERS + 1)
        ]
        first = f // band_local * (band_local * 8 * planes) + f % band_local
        out_ref[pl.ds(first, 8 * planes, stride=band_local), :] = functools.reduce(jnp.add, terms)


def body(size, start, energies, sites, potential):
    grids, bands, fields, planes, band_local, _ = size
    slabs = fields // band_local
    flat = (fields * planes * 8, 128)

    def flatten(x):
        return x.reshape(slabs, band_local, 8 * planes, 128).transpose(0, 2, 1, 3).reshape(flat)

    vmem = pl.BlockSpec(memory_space=pltpu.VMEM)
    anywhere = pl.BlockSpec(memory_space=pltpu.HBM)
    dma = pltpu.SemaphoreType.DMA
    constants = tables()
    plane_rows, basis = pl.pallas_call(
        functools.partial(exchange_kernel, size),
        out_shape=(
            pltpu.VMEM((2 * fields, 1, 128), F32),
            pltpu.VMEM((fields, ITERS + 1, planes, 8, 128), F32),
        ),
        in_specs=[anywhere] * 9,
        out_specs=(vmem, vmem),
        scratch_shapes=[
            pltpu.VMEM(flat, F32),
            pltpu.VMEM(flat, F32),
            pltpu.SMEM((1, 3), jnp.int32),
        ]
        + [pltpu.VMEM(c.shape, c.dtype) for c in constants]
        + [
            pltpu.VMEM((fields, planes, 8, 128), F32),
            pltpu.VMEM((GRIDN, 8, 128), F32),
            pltpu.VMEM((GRIDN, 8, 128), F32),
            pltpu.VMEM((GRIDN, 2 * GRIDN, GRIDN), F32),
            pltpu.VMEM((ROWS, 128), F32),
            pltpu.VMEM((ITERS, GRIDN, 8, 128), F32),
            pltpu.VMEM((bands // 2, 1, 128), F32),
            dma((10,)),
        ]
        + [dma] * 10,
        compiler_params=pltpu.CompilerParams(
            collective_id=0, has_side_effects=True, vmem_limit_bytes=60 * 1024 * 1024
        ),
    )(flatten(start), flatten(energies), sites.T, potential, *constants)
    out, alphas, betas = pl.pallas_call(
        functools.partial(merge_kernel, size),
        out_shape=(
            jax.ShapeDtypeStruct(flat, F32),
            jax.ShapeDtypeStruct((1, 1, ITERS), F32),
            jax.ShapeDtypeStruct((1, 1, ITERS), F32),
        ),
        in_specs=[vmem, vmem],
        out_specs=(vmem, vmem, vmem),
        compiler_params=pltpu.CompilerParams(vmem_limit_bytes=16 * 1024 * 1024),
    )(plane_rows, basis)
    out = out.reshape(slabs, 8 * planes, band_local, 128).transpose(0, 2, 1, 3)
    return alphas, betas, out.reshape(start.shape)


def solution(mesh):
    grids, bands = mesh.shape["grid"], mesh.shape["band"]

    def whole(start, energies, sites, potential):
        atoms, cores, pols, band_count, points = start.shape
        band_local = band_count // bands
        size = (grids, bands, cores * band_local, GRIDN // grids, band_local, cores * band_count * points)
        return jax.shard_map(
            functools.partial(body, size),
            mesh=mesh,
            in_specs=(P(None, None, None, "band", "grid"), P(None, "band", "grid"), P(), P()),
            out_specs=(P(), P(), P(None, None, None, "band", "grid")),
            check_vma=False,
        )(start, energies, sites, potential)

    return whole
```

time: 53.2 us -> 42 us (0.79)
  local copies, waits for them, and re-layouts: 6.71 us -> 0 us
  Pallas kernels: 45.6 us -> 41.2 us
    pallas_call x1 -> x2, Pallas kernels: 45.6 us -> 41.2 us  [the longest x1 39.7 us: body(): pl.pallas_call(functools.partial(exchange_kernel, size), out_shape=(pltpu...]
    reshape x3 -> x0, local copies, waits for them, and re-layouts: 3.66 us -> none  [the longest x1 1.53 us: body(): start.reshape(slab)]
    unnamed x9 -> x0, local copies, waits for them, and re-layouts: 3.05 us -> none
where the time goes in v2:
time: 42 us; the launch traced here: 41.8 us
  Pallas kernels  41.2 us (98%)
  between operations  0.64 us (2%)
    pallas_call x1, Pallas kernels, body(): pl.pallas_call(functools.partial(exchange_kernel, size), out_shape=(pltpu...  39.7 us
    pallas_call x1, Pallas kernels, body(): pl.pallas_call(functools.partial(merge_kernel, size), out_shape=(jax.Shap...  1.51 us

profile of v2, /device:TPU:1, one launch (start us, length us, event | category | flops | bytes accessed | tf_op | source)
XLA Modules:
  0.0 41.8 jit_solution(996006377713500810)
XLA Ops:
  0.6 39.7 %shard_map.112 = (f32[32,1,128]{2,1,0:T(1,128)S(1)}, f32[16,5,1,8,128]{4,3,2,1,0:T(8,128)S(1)}) custom-call(f32[128,128]{1,0:T(8,128)} %bitcast.16, f32[128,128]{1,0:T(8,128)} %bitcast.17, s32[1,3]{1,0:T(1,128)} %bitcast.18, f32[32,32,32]{2,1,0:T(8,128)} %potential_ref.1, bf16[2,512,256]{2,1,0:T(8,128)(2,1)} %constant.23.left_hbm, ...), custom_call_target="tpu_custom_call" | custom-call | tf_op jit(solution)/shard_map/pallas_call | solution.py:418
  40.3 1.5 %shard_map.113 = (f32[128,128]{1,0:T(8,128)}, f32[1,1,4]{2,1,0:T(1,128)}, f32[1,1,4]{2,1,0:T(1,128)}) custom-call(f32[32,1,128]{2,1,0:T(1,128)S(1)} %get-tuple-element.8.plane_buf, f32[16,5,1,8,128]{4,3,2,1,0:T(8,128)S(1)} %get-tuple-element.9.basis), custom_call_target="tpu_custom_call" | custom-call | tf_op jit(solution)/shard_map/pallas_call | solution.py:447
